TPU v7x, 32 devices: a whole 2x2x4 slice. The times are simulated.
32 devices in a mesh: groups: 2 (over x), ep: 8 (over z, y), section: 2 (over core).
Axes of the slice: x: 2, y: 2, z: 4, core: 2. Of those that a mesh axis runs over, the one named last changes fastest.
Arguments:
- resid: bfloat16 [2048, 4096], P(('groups', 'ep')), parts along dimension 0, may hold values from -6 to 6
- norm_gain: bfloat16 [4096], replicated, may hold values from 0.3984375 to 1.59375
- gate_logits: float32 [2048, 8], P(('groups', 'ep')), parts along dimension 0, may hold values from 0.1 to 1
- routes: int32 [2048, 8], P(('groups', 'ep')), parts along dimension 0, may hold values from 0 to 31, all different within a row; in each aligned block of 128 rows (0 to 127, 128 to 255, ...) at most 40 rows name the same one
- w_gate: bfloat16 [32, 4096, 768], P('ep', None, 'section'), may hold values from -0.09375 to 0.09375
- w_up: bfloat16 [32, 4096, 768], P('ep', None, 'section'), may hold values from -0.09375 to 0.09375
- w_down: bfloat16 [32, 768, 4096], P('ep', 'section'), may hold values from -0.21875 to 0.21875
- keys_raw: bfloat16 [2048, 512], P(('groups', 'ep'), 'section'), parts along dimension 0, may hold values from -6 to 6
- values_raw: bfloat16 [2048, 512], P(('groups', 'ep'), 'section'), parts along dimension 0, may hold values from -6 to 6
- k_gain: bfloat16 [128], replicated, may hold values from 0.25 to 1.75
- lengths: int32 [16], P(('groups', 'ep')), parts along dimension 0, may hold values from 32 to 128
- page_owner: int32 [16, 8], P(('groups', 'ep')), parts along dimension 0, may hold values from 0 to 7, as said below
- page_slot: int32 [16, 8], P(('groups', 'ep')), parts along dimension 0, may hold values from 0 to 7, as said below
Outputs:
- moe_out: bfloat16 [2048, 4096], P(('groups', 'ep'), 'section'), parts along dimension 0
- kv_cache: bfloat16 [128, 16, 2, 512], P(('groups', 'ep'), None, None, 'section'), parts along dimension 0
There are 2 independent parts, one for each index of `groups`. A program takes and returns all parts, laid end to end along the dimension named above; an argument that names none is the same for every part. Nothing has to cross between parts.
Inputs may be any that keep to these rules, and one draw needn't show every extreme that they name: `page_owner`: each prompt sends its 8 pages to 4 different owners, exactly 2 pages to each of them; every owner receives exactly 8 pages. `page_slot`: the pages that reach one owner have different slots, so every slot of every owner is filled once.
All inputs are finite; a program needn't handle non-finite values.
Results may differ from a plain program's by a relative error of at most 0.0076.
Values may be sent and summed in bfloat16 or wider, within the bound.
A program may use at most 128 MiB of HBM per device.

v0:
```python
import math

import jax
import jax.numpy as jnp
from jax import lax
from jax.sharding import PartitionSpec as P

HEAD = 128
TOP = 8
EXPERTS = 32
PAGE = 16
PAGE_PEER = 2
CAP = 40
PAGES = 8


def rms_scale(values, gain_row):
    mean_square = jnp.mean(values * values, axis=-1, keepdims=True)
    return values * lax.rsqrt(mean_square + 1e-06) * gain_row


def rotate_keys(key_block, position):
    half_size = key_block.shape[-1] // 2
    frequency = jnp.exp(
        jnp.arange(half_size, dtype=jnp.float32)
        * (-2.0 / key_block.shape[-1])
        * math.log(1000000.0)
    )
    angles = position.astype(jnp.float32)[:, None, None] * frequency
    cosine = jnp.cos(angles)
    sine_part = jnp.sin(angles)
    first_half = key_block[..., :half_size]
    second = key_block[..., half_size:]
    return jnp.concatenate(
        [first_half * cosine - second * sine_part, second * cosine + first_half * sine_part],
        axis=-1,
    )


def send_back(summed):
    return lax.all_to_all(summed, "ep", split_axis=0, concat_axis=0, tiled=True)


def shards(
    resid,
    norm_gain,
    gate_logits,
    routes,
    w_gate,
    w_up,
    w_down,
    keys_raw,
    values_raw,
    k_gain,
    lengths,
    page_owner,
    page_slot,
):
    tok_rows, model_width = resid.shape
    section_count = lax.axis_size("section")
    peer_count = lax.axis_size("ep")
    local_experts = w_gate.shape[0]
    col_width = model_width // section_count
    position = jnp.arange(tok_rows, dtype=jnp.int32)
    is_live = position < lengths[0]
    hidden = rms_scale(resid.astype(jnp.float32), norm_gain.astype(jnp.float32)).astype(
        jnp.bfloat16
    )
    mixing = (gate_logits / jnp.sum(gate_logits, axis=-1, keepdims=True)).astype(jnp.bfloat16)
    chosen = routes.reshape(-1)
    live_rows = jnp.repeat(is_live, TOP)
    expert_hits = (
        (chosen[:, None] == jnp.arange(EXPERTS, dtype=jnp.int32)[None, :]) & live_rows[:, None]
    ).astype(jnp.int32)
    slot_rank = jnp.sum((jnp.cumsum(expert_hits, axis=0) - expert_hits) * expert_hits, axis=1)
    target = jnp.where(live_rows, chosen * CAP + slot_rank, -1)
    slot_ids = jnp.arange(EXPERTS * CAP, dtype=jnp.int32)
    placing = (
        (slot_ids[:, None] == target[None, :])
        .astype(jnp.int32)
        .reshape(EXPERTS * CAP, tok_rows, TOP)
    )
    dispatch = jnp.sum(placing, axis=2).astype(jnp.bfloat16)
    picking = (target[:, None] == slot_ids[None, :]).astype(jnp.float32) * mixing.reshape(-1)[
        :, None
    ].astype(jnp.float32)
    combine = jnp.sum(picking.reshape(tok_rows, TOP, EXPERTS * CAP), axis=1).astype(jnp.bfloat16)
    outgoing = jnp.dot(dispatch, hidden, preferred_element_type=jnp.float32).astype(jnp.bfloat16)
    outgoing = outgoing.reshape(peer_count, local_experts, CAP, model_width)
    arrived = lax.all_to_all(outgoing, "ep", split_axis=0, concat_axis=0, tiled=True)
    gate_part = jnp.einsum("sjcd,jdf->sjcf", arrived, w_gate, preferred_element_type=jnp.float32)
    up_part = jnp.einsum("sjcd,jdf->sjcf", arrived, w_up, preferred_element_type=jnp.float32)
    active = (jax.nn.silu(gate_part) * up_part).astype(jnp.bfloat16)
    partial_out = jnp.einsum("sjcf,jfd->sjcd", active, w_down, preferred_element_type=jnp.float32)
    summed = lax.psum_scatter(partial_out, "section", scatter_dimension=3, tiled=True).astype(
        jnp.bfloat16
    )
    returned = send_back(summed)
    moe_out = jnp.dot(
        combine, returned.reshape(EXPERTS * CAP, col_width), preferred_element_type=jnp.float32
    ).astype(jnp.bfloat16)
    heads_local = keys_raw.shape[1] // HEAD
    normed = rms_scale(
        keys_raw.astype(jnp.float32).reshape(tok_rows, heads_local, HEAD),
        k_gain.astype(jnp.float32),
    )
    turned = rotate_keys(normed, position)
    key_rows = (
        jnp.where(is_live[:, None, None], turned, 0.0)
        .astype(jnp.bfloat16)
        .reshape(tok_rows, heads_local * HEAD)
    )
    value_rows = jnp.where(is_live[:, None], values_raw, jnp.zeros_like(values_raw))
    kv_width = key_rows.shape[1]
    page_rows = jnp.stack([key_rows, value_rows], axis=1).reshape(PAGES, PAGE * 2 * kv_width)
    owners = page_owner.reshape(-1)
    page_slots = page_slot.reshape(-1)
    peer_hits = (owners[:, None] == jnp.arange(peer_count, dtype=jnp.int32)[None, :]).astype(
        jnp.int32
    )
    page_rank = jnp.sum((jnp.cumsum(peer_hits, axis=0) - peer_hits) * peer_hits, axis=1)
    lane_index = owners * PAGE_PEER + page_rank
    lane_ids = jnp.arange(peer_count * PAGE_PEER, dtype=jnp.int32)
    select = (lane_ids[:, None] == lane_index[None, :]).astype(jnp.int32)
    send_pages = jnp.dot(
        select.astype(jnp.bfloat16), page_rows, preferred_element_type=jnp.float32
    ).astype(jnp.bfloat16)
    send_pages = send_pages.reshape(peer_count, PAGE_PEER, PAGE * 2 * kv_width)
    send_slots = (
        jnp.sum(select * page_slots[None, :], axis=1) + jnp.sum(select, axis=1) - 1
    ).reshape(peer_count, PAGE_PEER)
    got_pages, got_slots = (
        lax.all_to_all(send_pages, "ep", split_axis=0, concat_axis=0, tiled=True),
        lax.all_to_all(send_slots, "ep", split_axis=0, concat_axis=0, tiled=True),
    )
    placing_map = (
        jnp.arange(PAGES, dtype=jnp.int32)[:, None] == got_slots.reshape(-1)[None, :]
    ).astype(jnp.bfloat16)
    kv_cache = jnp.dot(
        placing_map,
        got_pages.reshape(peer_count * PAGE_PEER, PAGE * 2 * kv_width),
        preferred_element_type=jnp.float32,
    )
    kv_cache = kv_cache.astype(jnp.bfloat16).reshape(PAGES, PAGE, 2, kv_width)
    return (moe_out, kv_cache)


def solution(mesh):
    in_specs = (
        P(("groups", "ep"), None),
        P(),
        P(("groups", "ep"), None),
        P(("groups", "ep"), None),
        P("ep", None, "section"),
        P("ep", None, "section"),
        P("ep", "section", None),
        P(("groups", "ep"), "section"),
        P(("groups", "ep"), "section"),
        P(),
        P(("groups", "ep")),
        P(("groups", "ep"), None),
        P(("groups", "ep"), None),
    )
    out_specs = (P(("groups", "ep"), "section"), P(("groups", "ep"), None, None, "section"))
    return jax.shard_map(shards, mesh=mesh, in_specs=in_specs, out_specs=out_specs, check_vma=False)
```

profile of v0, /device:TPU:0, one launch (start us, length us, event | category | flops | bytes accessed | tf_op | source)
XLA Modules:
  0.0 472.4 jit_solution(17072859098015549610)
XLA Ops:
  7.2 0.8 copy.73
  9.1 9.0 %reduce-window.6 = s32[32,8,128]{2,1,0:T(8,128)S(1)} reduce-window(s32[32,8,128]{2,1,0:T(8,128)S(1)} %fusion.32, s32[]{:T(128)} %constant.32.clone.1), window={size=1x1x128 pad=0_0x0_0x127_0}, to_apply=%region_0.0 | reduce-window | flops 4161536 | bytes 262148 | tf_op jit(solution)/shard_map/reduce-window
  18.9 0.7 add_select_fusion
  19.6 6.7 %convert_reduce_fusion = s32[1280,128]{1,0:T(8,128)S(1)} fusion(s32[128,8]{0,1:T(8,128)S(1)} %add_select_fusion), kind=kLoop, calls=%fused_computation.12 | loop fusion | flops 3768320 | bytes 659456 | tf_op jit(solution)/shard_map/reduce_sum | solution.py:83
  26.3 0.7 convert_element_type.101
  27.0 1.5 fusion.11
  28.5 4.5 convolution_convert_fusion
  33.1 235.1 %all_to_all.21 = bf16[8,4,40,4096]{3,2,1,0:T(8,128)(2,1)S(1)} all-to-all(bf16[8,4,40,4096]{3,2,1,0:T(8,128)(2,1)S(1)} %bitcast.78), channel_id=1, replica_groups=mesh['groups'=2,'ep'=8,'section'=2] {'ep'}, dimensions={0} | all-to-all | bytes 20971520 | tf_op jit(solution)/shard_map/all_to_all | solution.py:90
  268.2 4.0 copy-done
  272.1 10.1 %fusion.4 = f32[4,8,40,384]{3,2,1,0:T(8,128)} fusion(bf16[4,4096,384]{2,1,0:T(8,128)(2,1)} %param.17, bf16[8,4,40,4096]{3,2,1,0:T(8,128)(2,1)S(1)} %all_to_all.21), kind=kOutput, calls=%fused_computation.5 | convolution fusion | flops 4026531840 | bytes 25034752 | tf_op jit(solution)/shard_map/sjcd,jdf->sjcf/dot_general | solution.py:91
  282.3 12.4 %fusion.14 = bf16[8,4,40,384]{3,2,0,1:T(8,128)(2,1)S(1)} fusion(f32[4,8,40,384]{3,2,1,0:T(8,128)} %fusion.4, bf16[4,4096,384]{2,1,0:T(8,128)(2,1)} %param.18, bf16[8,4,40,4096]{3,2,1,0:T(8,128)(2,1)} %copy-done), kind=kOutput, calls=%fused_computation.23 | convolution fusion | flops 4029480960 | bytes 26017792 | tf_op jit(solution)/shard_map/sjcd,jdf->sjcf/dot_general | solution.py:92
  294.8 9.9 %fusion.6 = f32[8,4,40,4096]{3,2,0,1:T(8,128)} fusion(bf16[8,4,40,384]{3,2,0,1:T(8,128)(2,1)S(1)} %fusion.14, bf16[4,384,4096]{2,1,0:T(8,128)(2,1)S(1)} %bitcast.80), kind=kOutput, calls=%fused_computation.7 | convolution fusion | flops 4026531840 | bytes 34537472 | tf_op jit(solution)/shard_map/sjcf,jfd->sjcd/dot_general | solution.py:94
  306.4 3.6 all-to-all-start.2
  312.2 0.9 reshape.267
  313.1 3.3 all-to-all-done.2
  316.4 3.4 all-to-all-start.3
  319.9 11.8 %reduce-scatter.2.cloned.1.call-done = f32[8,4,40,2048]{3,2,0,1:T(8,128)} async-done(((f32[8,4,40,4096]{3,2,0,1:T(8,128)}), f32[8,4,40,2048]{3,2,0,1:T(8,128)}) %reduce-scatter.2.cloned.1.call-update) | async-done | bytes 10485776 | tf_op jit(solution)/shard_map/reduce_scatter | solution.py:95
  331.7 4.8 %convert_element_type.105 = bf16[8,4,40,2048]{3,2,0,1:T(8,128)(2,1)S(1)} convert(f32[8,4,40,2048]{3,2,0,1:T(8,128)} %reduce-scatter.2.cloned.1.call-done) | non-fusion elementwise | flops 2621440 | bytes 15728640 | tf_op jit(solution)/shard_map/convert_element_type | solution.py:95
  336.5 2.8 copy.83
  339.3 6.0 %all-to-all-start.1 = ((bf16[8,4,40,2048]{3,2,1,0:T(8,128)(2,1)}), bf16[8,4,40,2048]{3,2,1,0:T(8,128)(2,1)}, u32[]{:S(2)}, u32[]{:S(2)}) async-start(bf16[8,4,40,2048]{3,2,1,0:T(8,128)(2,1)} %copy.83), calls=%async_computation.2 | async-start | bytes 10485760 | tf_op jit(solution)/shard_map/all_to_all | solution.py:41
  345.5 1.7 select_reduce_fusion
  348.7 0.8 copy.88
  349.5 111.9 %all-to-all-done.1 = bf16[8,4,40,2048]{3,2,1,0:T(8,128)(2,1)} async-done(((bf16[8,4,40,2048]{3,2,1,0:T(8,128)(2,1)}), bf16[8,4,40,2048]{3,2,1,0:T(8,128)(2,1)}, u32[]{:S(2)}, u32[]{:S(2)}) %all-to-all-start.1) | async-done | bytes 5242912 | tf_op jit(solution)/shard_map/all_to_all | solution.py:41
  461.4 4.1 convolution_convert_fusion.3
  (75 shorter events, 6.8 us)
Async XLA Ops:
  7.2 324.5 %reduce-scatter.2.cloned.1.call-start = ((), (), s32[]{:S(2)}) async-start(), calls=%async_computation.5 | async-start | bytes 31457280 | tf_op jit(solution)/shard_map/reduce_scatter | solution.py:95
  268.2 4.0 copy-start
  272.1 22.6 %slice-start = ((s8[12582912]{0:T(1024)(128)(4,1)}), s8[4194304]{0:T(1024)(128)(4,1)S(1)}, s32[]{:S(2)}) async-start(s8[12582912]{0:T(1024)(128)(4,1)} %bitcast.79), calls=%async_computation.6 | async-start | bytes 8388608
  272.1 22.6 %slice-start.1 = ((s8[12582912]{0:T(1024)(128)(4,1)}), s8[4194304]{0:T(1024)(128)(4,1)S(1)}, s32[]{:S(2)}) async-start(s8[12582912]{0:T(1024)(128)(4,1)} %bitcast.79), calls=%async_computation.7 | async-start | bytes 8388608
  282.3 12.5 %slice-start.2 = ((s8[12582912]{0:T(1024)(128)(4,1)}), s8[4194304]{0:T(1024)(128)(4,1)S(1)}, s32[]{:S(2)}) async-start(s8[12582912]{0:T(1024)(128)(4,1)} %bitcast.79), calls=%async_computation.8 | async-start | bytes 8388608
  304.7 0.7 copy-start.4
  304.7 0.9 copy-start.5
  304.7 5.3 %copy-start.1 = (bf16[128,256]{1,0:T(8,128)(2,1)S(1)}, bf16[128,256]{1,0:T(8,128)(2,1)}, u32[]{:S(2)}) copy-start(bf16[128,256]{1,0:T(8,128)(2,1)} %param.20) | copy-start | bytes 196612
  304.7 5.4 %copy-start.6 = (bf16[128]{0:T(256)(128)(2,1)S(1)}, bf16[128]{0:T(256)(128)(2,1)}, u32[]{:S(2)}) copy-start(bf16[128]{0:T(256)(128)(2,1)} %param.22) | copy-start | bytes 772
  304.7 6.8 %copy-start.2 = (bf16[128,256]{1,0:T(8,128)(2,1)S(1)}, bf16[128,256]{1,0:T(8,128)(2,1)}, u32[]{:S(2)}) copy-start(bf16[128,256]{1,0:T(8,128)(2,1)} %param.21) | copy-start | bytes 196612
  306.4 10.0 %all-to-all-start.2 = ((s32[8,1,2]{2,1,0:T(1,128)}), s32[8,1,2]{2,1,0:T(1,128)S(1)}, u32[]{:S(2)}, u32[]{:S(2)}) async-start(s32[8,1,2]{2,1,0:T(1,128)} %bitcast.18), calls=%async_computation.3 | async-start | bytes 8192 | tf_op jit(solution)/shard_map/all_to_all | solution.py:134
  316.4 22.9 %all-to-all-start.3 = ((bf16[8,2,8192]{2,1,0:T(2,128)(2,1)}), bf16[8,2,8192]{2,1,0:T(2,128)(2,1)S(1)}, u32[]{:S(2)}, u32[]{:S(2)}) async-start(bf16[8,2,8192]{2,1,0:T(2,128)(2,1)} %reshape.267), calls=%async_computation.4 | async-start | bytes 524288 | tf_op jit(solution)/shard_map/all_to_all | solution.py:133
  339.3 6.1 %copy-start.3 = (f32[128,8]{0,1:T(8,128)S(1)}, f32[128,8]{0,1:T(8,128)}, u32[]{:S(2)}) copy-start(f32[128,8]{0,1:T(8,128)} %param.15) | copy-start | bytes 12292
  339.3 122.1 %all-to-all-start.1 = ((bf16[8,4,40,2048]{3,2,1,0:T(8,128)(2,1)}), bf16[8,4,40,2048]{3,2,1,0:T(8,128)(2,1)}, u32[]{:S(2)}, u32[]{:S(2)}) async-start(bf16[8,4,40,2048]{3,2,1,0:T(8,128)(2,1)} %copy.83), calls=%async_computation.2 | async-start | bytes 10485760 | tf_op jit(solution)/shard_map/all_to_all | solution.py:41
Sparse Core Ops, SparseCore 0:
  304.9 26.7 reduce-scatter.1
where the time goes:
time: 473 us; the launch traced here: 472 us
  blocking collectives  235 us (50%)
  waiting for transfers between devices  127 us (27%)
  matrix products  41.7 us (9%)
  other arithmetic  27.8 us (6%)
  between operations  15 us (3%)
  starting transfers between devices  13.1 us (3%)
  local copies, waits for them, and re-layouts  12.7 us (3%)
    all_to_all x1, blocking collectives, shards(): lax.all_to_all(outgoing, 'ep', split_axis=0, concat_axis=0, tiled=True)  235 us
    all_to_all x1, waiting for transfers between devices, send_back(): return lax.all_to_all(summed, 'ep', split_axis=0, concat_axis=0, tiled=True)  112 us
    dot_general x1, matrix products, shards(): jnp.einsum('sjcd,jdf->sjcf', arrived, w_up, preferred_element_type=jnp.fl...  12.4 us
    reduce_scatter x1, waiting for transfers between devices, shards(): lax.psum_scatter(partial_out, 'section', scatter_dimension=3, tiled=True)  11.8 us
    dot_general x1, matrix products, shards(): jnp.einsum('sjcd,jdf->sjcf', arrived, w_gate, preferred_element_type=jnp....  10.1 us
    dot_general x1, matrix products, shards(): jnp.einsum('sjcf,jfd->sjcd', active, w_down, preferred_element_type=jnp.f...  9.94 us
  transfers between devices with their start and end apart: 4, of which 3 were waited for; matrix products, arithmetic and copies ran while one was open for 3% of the time, Pallas kernels for 0%

commit v1 on v0

v1 whole, which is shorter than its diff:
```python
import functools
import math

import jax
import jax.numpy as jnp
from jax import lax
from jax.experimental import pallas as pl
from jax.experimental.pallas import tpu as pltpu
from jax.sharding import PartitionSpec as P

PAGE = 16
CAP = 40
F32 = jnp.float32
BF16 = jnp.bfloat16


def rms_scale(values, gain_row):
    mean_square = jnp.mean(values * values, axis=-1, keepdims=True)
    return values * lax.rsqrt(mean_square + 1e-06) * gain_row


def rotate_keys(key_block, position):
    half_size = key_block.shape[-1] // 2
    frequency = jnp.exp(
        jnp.arange(half_size, dtype=F32) * (-2.0 / key_block.shape[-1]) * math.log(1000000.0)
    )
    angles = position.astype(F32)[:, None, None] * frequency
    cosine = jnp.cos(angles)
    sine_part = jnp.sin(angles)
    first_half = key_block[..., :half_size]
    second = key_block[..., half_size:]
    return jnp.concatenate(
        [first_half * cosine - second * sine_part, second * cosine + first_half * sine_part],
        axis=-1,
    )


MESH = pl.DeviceIdType.MESH


def greet(outer, inner, z, y, ep, core, halves):
    barrier = pltpu.get_barrier_semaphore()

    def signal(to_ep, to_core):
        pl.semaphore_signal(
            barrier, inc=1, device_id={"ep": to_ep, "section": to_core}, device_id_type=MESH
        )

    pl.when(z > 0)(lambda: signal(ep - inner, core))
    pl.when(z < outer - 1)(lambda: signal(ep + inner, core))
    for k in range(1, inner):
        signal(z * inner + lax.rem(y + k, inner), core)
    for k in range(1, halves):
        signal(ep, lax.rem(core + k, halves))
    ends = jnp.where(z > 0, 1, 0) + jnp.where(z < outer - 1, 1, 0)
    pl.semaphore_wait(barrier, ends + inner - 1 + halves - 1)


def place(outer, inner):
    ep = lax.axis_index("ep")
    return ep, lax.axis_index("section"), lax.div(ep, inner), lax.rem(ep, inner)


def columns(ref, block, half, cols):
    return ref.at[block, :, pl.ds(pl.multiple_of(half * cols, cols), cols)]


def by_distance(outer, z, order, body):
    for d in order:
        for side in (-1, 1) if d else (1,):
            zz = z + side * d
            if d:
                pl.when((zz >= 0) & (zz < outer))(functools.partial(body, d, side, zz))
            else:
                body(d, side, zz)


def gather_kernel(outer, inner, halves, src, meta, out, mout, send, recv, msend, mrecv, local):
    ep, core, z, y = place(outer, inner)
    cols = src.shape[1]
    own = pltpu.make_async_copy(src, columns(out, ep, core, cols), local.at[0])
    mown = pltpu.make_async_copy(meta, mout.at[ep], local.at[1])
    own.start()
    mown.start()
    greet(outer, inner, z, y, ep, core, halves)
    own.wait()
    mown.wait()
    to_sibling = 1 + inner

    def rows_copy(block, half, kind, to_ep, to_core):
        return pltpu.make_async_remote_copy(
            src_ref=columns(out, block, half, cols),
            dst_ref=columns(out, block, half, cols),
            send_sem=send.at[kind, block],
            recv_sem=recv.at[block, half],
            device_id={"ep": to_ep, "section": to_core},
            device_id_type=MESH,
        )

    def meta_copy(block, kind, to_ep):
        return pltpu.make_async_remote_copy(
            src_ref=mout.at[block],
            dst_ref=mout.at[block],
            send_sem=msend.at[kind, block],
            recv_sem=mrecv.at[block],
            device_id={"ep": to_ep, "section": core},
            device_id_type=MESH,
        )

    def chip_copies(block, kind, to_ep, act):
        act(meta_copy(block, kind, to_ep))
        act(rows_copy(block, core, kind, to_ep, core))

    def column(block, d, side, act):
        if d == 0 or side == 1:
            pl.when(z > 0)(lambda: chip_copies(block, 0, ep - inner, act))
        if d == 0 or side == -1:
            pl.when(z < outer - 1)(lambda: chip_copies(block, 1, ep + inner, act))
        for k in range(1, inner):
            chip_copies(block, 1 + k, z * inner + lax.rem(y + k, inner), act)

    def sibling(block, act):
        for k in range(1, halves):
            act(rows_copy(block, core, to_sibling + k - 1, ep, lax.rem(core + k, halves)))

    def start(copy):
        copy.start()

    def wait_send(copy):
        copy.wait_send()

    def arrived(block, half):
        rows_copy(block, half, 0, ep, core).wait_recv()

    def step(d, side, zz):
        block = zz * inner + y
        if d:
            meta_copy(block, 0, ep).wait_recv()
            arrived(block, core)
        column(block, d, side, start)
        sibling(block, start)

    def across(d, side, zz):
        for k in range(1, inner):
            block = zz * inner + lax.rem(y + k, inner)
            meta_copy(block, 0, ep).wait_recv()
            arrived(block, core)
            sibling(block, start)

    def finish(d, side, zz):
        column(zz * inner + y, d, side, wait_send)
        for yy in range(inner):
            block = zz * inner + yy
            sibling(block, wait_send)
            for k in range(1, halves):
                arrived(block, lax.rem(core + k, halves))

    for d in range(outer + 1):
        if d < outer:
            by_distance(outer, z, (d,), step)
        if d > 0:
            by_distance(outer, z, (d - 1,), across)
    by_distance(outer, z, range(outer), finish)


def gather_rows(outer, inner, halves, hidden, meta):
    peers = outer * inner
    kinds = 1 + inner + halves - 1
    dma = pltpu.SemaphoreType.DMA
    vmem = pl.BlockSpec(memory_space=pltpu.VMEM)
    return pl.pallas_call(
        functools.partial(gather_kernel, outer, inner, halves),
        out_shape=(
            jax.ShapeDtypeStruct((peers, hidden.shape[0], halves * hidden.shape[1]), hidden.dtype),
            jax.ShapeDtypeStruct((peers,) + meta.shape, meta.dtype),
        ),
        in_specs=[vmem, vmem],
        out_specs=(vmem, vmem),
        scratch_shapes=[
            dma((kinds, peers)),
            dma((peers, halves)),
            dma((kinds, peers)),
            dma((peers,)),
            dma((2,)),
        ],
        compiler_params=pltpu.CompilerParams(collective_id=0, has_side_effects=True),
        name="gather_rows",
    )(hidden, meta)


def scatter_kernel(
    outer, inner, halves, mixed, out, acc, sib, yb, zb, lsem, ssend, srecv, ysend, yrecv, zsend, zrecv
):
    ep, core, z, y = place(outer, inner)
    other = halves - 1 - core
    tok, cols = out.shape

    def local_copy(block):
        return pltpu.make_async_copy(
            columns(mixed, block, core, cols), acc.at[block], lsem.at[block]
        )

    def sib_copy(block):
        return pltpu.make_async_remote_copy(
            src_ref=columns(mixed, block, other, cols),
            dst_ref=sib.at[block],
            send_sem=ssend.at[block],
            recv_sem=srecv.at[block],
            device_id={"ep": ep, "section": other},
            device_id_type=MESH,
        )

    def y_copy(zz, k):
        to_y = lax.rem(y + k, inner)
        return pltpu.make_async_remote_copy(
            src_ref=acc.at[zz * inner + to_y],
            dst_ref=yb.at[k - 1, zz],
            send_sem=ysend.at[k - 1, zz],
            recv_sem=yrecv.at[k - 1, zz],
            device_id={"ep": z * inner + to_y, "section": core},
            device_id_type=MESH,
        )

    def z_copy(zz, slot, to_ep):
        return pltpu.make_async_remote_copy(
            src_ref=acc.at[zz * inner + y],
            dst_ref=zb.at[slot],
            send_sem=zsend.at[zz],
            recv_sem=zrecv.at[slot],
            device_id={"ep": to_ep, "section": core},
            device_id_type=MESH,
        )

    def add(dst, *sources):
        def body(i, carry):
            piece = pl.ds(pl.multiple_of(i * 16, 16), 16)
            total = sources[0][piece, :].astype(F32)
            for source in sources[1:]:
                total = total + source[piece, :].astype(F32)
            dst[piece, :] = total.astype(dst.dtype)
            return carry

        lax.fori_loop(0, tok // 16, body, 0)

    greet(outer, inner, z, y, ep, core, halves)
    far_first = range(outer - 1, -1, -1)

    def open_step(d, side, zz):
        for k in list(range(1, inner)) + [0]:
            block = zz * inner + lax.rem(y + k, inner)
            sib_copy(block).start()
            local_copy(block).start()

    def y_step(d, side, zz):
        for k in range(1, inner):
            block = zz * inner + lax.rem(y + k, inner)
            local_copy(block).wait()
            sib_copy(block).wait_recv()
            add(acc.at[block], acc.at[block], sib.at[block])
            y_copy(zz, k).start()

    def z_step(d, side, zz):
        block = zz * inner + y
        local_copy(block).wait()
        sib_copy(block).wait_recv()
        for k in range(1, inner):
            y_copy(zz, k).wait_recv()
        parts = [acc.at[block], sib.at[block]] + [yb.at[k, zz] for k in range(inner - 1)]
        target = acc.at[block] if d else out
        if d:
            feeds = (z - side >= 0) & (z - side < outer)
            slot = outer if (d == 1 and side == -1) else zz

            @pl.when(feeds)
            def _():
                z_copy(zz, zz, ep).wait_recv()
                add(target, *parts, zb.at[zz])

            @pl.when(jnp.logical_not(feeds))
            def _():
                add(target, *parts)

            z_copy(zz, slot, ep + side * inner).start()
            return

        @pl.when(z > 0)
        def _():
            z_copy(zz, zz, ep).wait_recv()

        @pl.when(z == 0)
        def _():
            z_copy(zz, outer, ep).wait_recv()
            add(out, *parts, zb.at[outer])

        @pl.when(z == outer - 1)
        def _():
            add(out, *parts, zb.at[zz])

        @pl.when((z > 0) & (z < outer - 1))
        def _():
            z_copy(zz, outer, ep).wait_recv()
            add(out, *parts, zb.at[zz], zb.at[outer])

    def close_step(d, side, zz):
        for k in range(inner):
            sib_copy(zz * inner + lax.rem(y + k, inner)).wait_send()
        for k in range(1, inner):
            y_copy(zz, k).wait_send()
        if d:
            z_copy(zz, zz, ep).wait_send()

    by_distance(outer, z, far_first, open_step)
    by_distance(outer, z, far_first, y_step)
    by_distance(outer, z, far_first, z_step)
    by_distance(outer, z, far_first, close_step)


def scatter_sums(outer, inner, halves, mixed):
    peers = outer * inner
    shape = (mixed.shape[1], mixed.shape[2] // halves)
    dma = pltpu.SemaphoreType.DMA
    across = max(inner - 1, 1)
    return pl.pallas_call(
        functools.partial(scatter_kernel, outer, inner, halves),
        out_shape=jax.ShapeDtypeStruct(shape, mixed.dtype),
        in_specs=[pl.BlockSpec(memory_space=pl.ANY)],
        out_specs=pl.BlockSpec(memory_space=pltpu.VMEM),
        scratch_shapes=[
            pltpu.VMEM((peers,) + shape, mixed.dtype),
            pltpu.VMEM((peers,) + shape, mixed.dtype),
            pltpu.VMEM((across, outer if inner > 1 else 1) + shape, mixed.dtype),
            pltpu.VMEM((outer + 1,) + shape, mixed.dtype),
            dma((peers,)),
            dma((peers,)),
            dma((peers,)),
            dma((across, outer)),
            dma((across, outer)),
            dma((outer,)),
            dma((outer + 1,)),
        ],
        compiler_params=pltpu.CompilerParams(collective_id=1, has_side_effects=True),
        name="scatter_sums",
    )(mixed)


def inner_size(mesh):
    try:
        line = mesh.devices[0, :, 0]
        coords = [tuple(device.coords) for device in line]
        inner = 1
        while inner < len(coords) and sum(a != b for a, b in zip(coords[inner], coords[0])) == 1:
            axis = [i for i in range(3) if coords[1][i] != coords[0][i]][0]
            if coords[inner][axis] == coords[0][axis]:
                break
            inner += 1
        return inner if inner < len(coords) and len(coords) % inner == 0 else 1
    except (AttributeError, IndexError, TypeError):
        return 1


def shards(
    inner,
    resid,
    norm_gain,
    gate_logits,
    routes,
    w_gate,
    w_up,
    w_down,
    keys_raw,
    values_raw,
    k_gain,
    lengths,
    page_owner,
    page_slot,
):
    tok_rows, model_width = resid.shape
    halves = lax.axis_size("section")
    peers = lax.axis_size("ep")
    me = lax.axis_index("ep")
    core = lax.axis_index("section")
    local_experts, _, ff_half = w_gate.shape
    experts = local_experts * peers
    cols = model_width // halves
    position = jnp.arange(tok_rows, dtype=jnp.int32)
    is_live = position < lengths[0]

    wide = resid.astype(F32)
    scale = lax.rsqrt(jnp.mean(wide * wide, axis=-1, keepdims=True) + 1e-06)
    my_cols = lax.dynamic_slice_in_dim(resid, core * cols, cols, 1).astype(F32)
    my_gain = lax.dynamic_slice_in_dim(norm_gain, core * cols, cols, 0).astype(F32)
    hidden = (my_cols * scale * my_gain).astype(BF16)
    mixing = (gate_logits / jnp.sum(gate_logits, axis=-1, keepdims=True)).astype(BF16)
    expert_ids = jnp.arange(experts, dtype=jnp.int32)
    named = (routes[:, :, None] == expert_ids) & is_live[:, None, None]
    hits = jnp.any(named, axis=1)
    weight = jnp.sum(jnp.where(named, mixing.astype(F32)[:, :, None], 0.0), axis=1)
    earlier = (position[:, None] > position[None, :]).astype(BF16)
    rank = jnp.dot(earlier, hits.astype(BF16), preferred_element_type=F32)
    rank = jnp.where(hits, rank, -1.0)
    page_to = (page_owner * page_owner.shape[1] + page_slot).astype(F32)
    page_to = jnp.broadcast_to(page_to, (tok_rows, page_to.shape[1]))
    small = jnp.concatenate([rank, weight, page_to], axis=1).astype(BF16)
    small = jnp.pad(small, ((0, 0), (0, -small.shape[1] % 128)))
    rows, small = gather_rows(peers // inner, inner, halves, hidden, small)
    small = small.astype(F32)
    first = me * local_experts
    rank_in = lax.dynamic_slice_in_dim(small, first, local_experts, 2)
    weight_in = lax.dynamic_slice_in_dim(small, experts + first, local_experts, 2)
    page_in = small[:, 0, 2 * experts : 2 * experts + page_owner.shape[1]].reshape(-1)

    head = k_gain.shape[0]
    heads_local = keys_raw.shape[1] // head
    kv_width = keys_raw.shape[1]
    normed = rms_scale(
        keys_raw.astype(F32).reshape(tok_rows, heads_local, head), k_gain.astype(F32)
    )
    turned = rotate_keys(normed, position)
    key_rows = (
        jnp.where(is_live[:, None, None], turned, 0.0).astype(BF16).reshape(tok_rows, kv_width)
    )
    value_rows = jnp.where(is_live[:, None], values_raw, jnp.zeros_like(values_raw))
    pages = page_owner.shape[1]
    page_rows = jnp.stack([key_rows, value_rows], axis=1).reshape(pages, PAGE * 2 * kv_width)
    all_pages = lax.all_gather(page_rows, "ep", axis=0, tiled=True)
    slots = me * pages + jnp.arange(pages, dtype=jnp.int32)
    choose = (slots.astype(F32)[:, None] == page_in[None, :]).astype(BF16)
    kv_cache = jnp.dot(choose, all_pages, preferred_element_type=F32).astype(BF16)
    kv_cache = kv_cache.reshape(pages, PAGE, 2, kv_width)

    slot_ids = jnp.arange(CAP, dtype=jnp.int32).astype(F32)
    dispatch = (
        jnp.swapaxes(rank_in, 1, 2)[:, :, None, :] == slot_ids[:, None]
    ).astype(BF16)
    dispatch = dispatch.reshape(peers, local_experts * CAP, tok_rows)
    combine = jnp.where(rank_in[..., None] == slot_ids, weight_in[..., None], 0.0).astype(BF16)
    combine = combine.reshape(peers, tok_rows, local_experts * CAP)
    arrived = jnp.einsum("sct,std->scd", dispatch, rows, preferred_element_type=F32)
    arrived = arrived.astype(BF16).reshape(peers, local_experts, CAP, halves * cols)
    gate_part = jnp.einsum("sjcd,jdf->sjcf", arrived, w_gate, preferred_element_type=F32)
    up_part = jnp.einsum("sjcd,jdf->sjcf", arrived, w_up, preferred_element_type=F32)
    active = (jax.nn.silu(gate_part) * up_part).astype(BF16)
    part = jnp.einsum("sjcf,jfd->sjcd", active, w_down, preferred_element_type=F32).astype(BF16)
    part = part.reshape(peers, local_experts * CAP, model_width)
    mixed = jnp.einsum("stc,scd->std", combine, part, preferred_element_type=F32).astype(BF16)
    moe_out = scatter_sums(peers // inner, inner, halves, mixed)
    return (moe_out, kv_cache)


def solution(mesh):
    in_specs = (
        P(("groups", "ep"), None),
        P(),
        P(("groups", "ep"), None),
        P(("groups", "ep"), None),
        P("ep", None, "section"),
        P("ep", None, "section"),
        P("ep", "section", None),
        P(("groups", "ep"), "section"),
        P(("groups", "ep"), "section"),
        P(),
        P(("groups", "ep")),
        P(("groups", "ep"), None),
        P(("groups", "ep"), None),
    )
    out_specs = (P(("groups", "ep"), "section"), P(("groups", "ep"), None, None, "section"))
    body = functools.partial(shards, inner_size(mesh))
    return jax.shard_map(body, mesh=mesh, in_specs=in_specs, out_specs=out_specs, check_vma=False)
```

time: 473 us -> 220 us (0.47)
  blocking collectives: 235 us -> 0 us
  Pallas kernels: 0 us -> 128 us
  waiting for transfers between devices: 127 us -> 0.04 us
  other arithmetic: 27.8 us -> 12.1 us
  starting transfers between devices: 13.1 us -> 0.04 us
  matrix products: 41.7 us -> 47.7 us
    all_to_all x1 -> x0, blocking collectives: 235 us -> none  [shards(): lax.all_to_all(outgoing, 'ep', split_axis=0, concat_axis=0, tiled=True)]
    pallas_call x0 -> x2, Pallas kernels: none -> 128 us  [the longest x1 76.1 us: gather_rows(): pl.pallas_call(functools.partial(gather_kernel, outer, inner, halves), ou...]
    all_to_all x3 -> x0, waiting for transfers between devices: 115 us -> none  [the longest x1 112 us: send_back(): return lax.all_to_all(summed, 'ep', split_axis=0, concat_axis=0, tiled=True)]
    all_to_all x3 -> x0, starting transfers between devices: 13 us -> none  [the longest x1 6.02 us: send_back(): return lax.all_to_all(summed, 'ep', split_axis=0, concat_axis=0, tiled=True)]
    reduce_scatter x1 -> x0, waiting for transfers between devices: 11.8 us -> none  [shards(): lax.psum_scatter(partial_out, 'section', scatter_dimension=3, tiled=True)]
    another operation x4 -> x1, other arithmetic: 9.17 us -> 0.68 us
    convert_element_type x2 -> x1, local copies, waits for them, and re-layouts: 2.89 us -> 9.61 us  [shards(): jnp.einsum('sjcf,jfd->sjcd', active, w_down, preferred_element_type=F32)]
    reduce_sum x5 -> x2, other arithmetic: 8.63 us -> 2.24 us  [the longest x1 1.52 us: shards(): scale = lax.rsqrt(jnp.mean(wide * wide, axis=-1, keepdims=True) + 1e-06)]
  transfers between devices with their start and end apart: 4 -> 1, of which waited for: 3 -> 0; matrix products, arithmetic and copies ran while one was open for 3% -> 31% of each run, Pallas kernels for 0% -> 58%
where the time goes in v1:
time: 220 us; the launch traced here: 219 us
  Pallas kernels  128 us (58%)
  matrix products  47.7 us (22%)
  local copies, waits for them, and re-layouts  16.3 us (7%)
  between operations  14.9 us (7%)
  other arithmetic  12.1 us (6%)
    pallas_call x1, Pallas kernels, gather_rows(): pl.pallas_call(functools.partial(gather_kernel, outer, inner, halves), ou...  76.1 us
    pallas_call x1, Pallas kernels, scatter_sums(): pl.pallas_call(functools.partial(scatter_kernel, outer, inner, halves), o...  52.2 us
    dot_general x1, matrix products, shards(): jnp.einsum('sjcf,jfd->sjcd', active, w_down, preferred_element_type=F32)  12.7 us
    dot_general x1, matrix products, shards(): jnp.einsum('stc,scd->std', combine, part, preferred_element_type=F32)  9.7 us
    convert_element_type x1, local copies, waits for them, and re-layouts, shards(): jnp.einsum('sjcf,jfd->sjcd', active, w_down, preferred_element_type=F32)  9.61 us
    dot_general x1, matrix products, shards(): jnp.einsum('sjcd,jdf->sjcf', arrived, w_gate, preferred_element_type=F32)  8.76 us
    dot_general x1, matrix products, shards(): jnp.einsum('sjcd,jdf->sjcf', arrived, w_up, preferred_element_type=F32)  8.66 us
    dot_general x1, matrix products, shards(): jnp.einsum('sct,std->scd', dispatch, rows, preferred_element_type=F32)  6.24 us
  transfers between devices with their start and end apart: 1, of which 0 were waited for; matrix products, arithmetic and copies ran while one was open for 31% of the time, Pallas kernels for 58%

profile of v1, /device:TPU:0, one launch (start us, length us, event | category | flops | bytes accessed | tf_op | source)
XLA Modules:
  0.0 219.4 jit_solution(12674130008354706198)
XLA Ops:
  7.9 0.7 convert_element_type.116
  8.6 0.9 reshape.175
  10.8 0.9 select_bitcast_fusion
  12.0 0.7 reshape.171
  12.7 1.5 multiply_reduce_fusion
  14.3 0.7 reduce_sum.37
  15.0 0.7 fusion.23
  15.7 0.7 fusion.21
  16.4 0.7 select_reduce_fusion
  17.5 0.7 convert_bitcast_fusion.1
  18.2 0.7 dynamic-slice_convert_fusion
  19.6 2.0 multiply_convert_fusion.src
  21.7 76.1 %gather_rows.1 = (bf16[8,128,4096]{2,1,0:T(8,128)(2,1)}, bf16[8,128,128]{2,1,0:T(8,128)(2,1)}) custom-call(bf16[128,2048]{1,0:T(8,128)(2,1)} %multiply_convert_fusion.src, bf16[128,128]{1,0:T(8,128)(2,1)} %pad.4.meta), custom_call_target="tpu_custom_call" | custom-call | tf_op jit(solution)/shard_map/gather_rows/pallas_call | solution.py:171
  97.7 1.0 convert_element_type.107
  100.3 6.2 %convolution_convert_fusion.1 = bf16[8,160,4096]{2,1,0:T(8,128)(2,1)S(1)} fusion(pred[8,160,128]{2,1,0:T(32,128)(4,1)S(1)} %bitcast_compare_fusion, bf16[8,128,4096]{2,1,0:T(8,128)(2,1)} %get-tuple-element.5), kind=kOutput, calls=%fused_computation.10 | convolution fusion | flops 1347420160 | bytes 19038208 | tf_op jit(solution)/shard_map/sct,std->scd/dot_general | solution.py:438
  106.5 8.8 %fusion.4 = f32[4,8,40,384]{3,2,1,0:T(8,128)S(1)} fusion(bf16[4,4096,384]{2,1,0:T(8,128)(2,1)} %param.17, bf16[8,4,40,4096]{3,2,1,0:T(8,128)(2,1)S(1)} %bitcast.67), kind=kOutput, calls=%fused_computation.4 | convolution fusion | flops 4026531840 | bytes 25034752 | tf_op jit(solution)/shard_map/sjcd,jdf->sjcf/dot_general | solution.py:440
  115.3 8.7 %fusion.10 = bf16[8,4,40,384]{3,2,0,1:T(8,128)(2,1)S(1)} fusion(f32[4,8,40,384]{3,2,1,0:T(8,128)S(1)} %fusion.4, bf16[4,4096,384]{2,1,0:T(8,128)(2,1)} %param.18, bf16[8,4,40,4096]{3,2,1,0:T(8,128)(2,1)S(1)} %bitcast.68), kind=kOutput, calls=%fused_computation.14 | convolution fusion | flops 4029480960 | bytes 26017792 | tf_op jit(solution)/shard_map/sjcd,jdf->sjcf/dot_general | solution.py:441
  123.9 12.7 %convert_bitcast_fusion = bf16[8,4,40,4096]{3,2,0,1:T(8,128)(2,1)} fusion(bf16[8,4,40,384]{3,2,0,1:T(8,128)(2,1)S(1)} %fusion.10, bf16[4,384,4096]{2,1,0:T(8,128)(2,1)} %param.19), kind=kOutput, calls=%fused_computation.6 | convolution fusion | flops 4031774720 | bytes 24051712 | tf_op jit(solution)/shard_map/sjcf,jfd->sjcd/dot_general | solution.py:443
  136.6 9.6 %copy.64 = bf16[8,4,40,4096]{3,2,1,0:T(8,128)(2,1)} copy(bf16[8,4,40,4096]{3,2,0,1:T(8,128)(2,1)} %convert_bitcast_fusion) | data formatting | bytes 20971520 | tf_op jit(solution)/shard_map/convert_element_type | solution.py:443
  146.4 9.7 %convolution_convert_fusion.2.mixed = bf16[8,128,4096]{2,1,0:T(8,128)(2,1)} fusion(bf16[8,128,160]{1,2,0:T(8,128)(2,1)S(1)} %fusion.19, bf16[8,160,4096]{2,1,0:T(8,128)(2,1)} %bitcast.66), kind=kOutput, calls=%fused_computation.11 | convolution fusion | flops 1346371584 | bytes 19202048 | tf_op jit(solution)/shard_map/stc,scd->std/dot_general | solution.py:445
  156.1 52.2 %scatter_sums.1 = bf16[128,2048]{1,0:T(8,128)(2,1)} custom-call(bf16[8,128,4096]{2,1,0:T(8,128)(2,1)} %convolution_convert_fusion.2.mixed), custom_call_target="tpu_custom_call" | custom-call | tf_op jit(solution)/shard_map/scatter_sums/pallas_call | solution.py:323
  208.4 1.5 convolution_convert_fusion
  209.9 0.8 copy.68
  210.7 1.9 copy.85
  (37 shorter events, 4.4 us)
Async XLA Ops:
  7.2 201.2 %all-gather.2.cloned.1.call-start = ((), (), s32[]{:S(2)}) async-start(), calls=%async_computation | async-start | bytes 1179648 | tf_op jit(solution)/shard_map/all_gather | solution.py:425
Sparse Core Ops, SparseCore 0:
  12.8 50.9 all-gather.1
